TPU v7x, 512 devices: a 8x2x16 block of a 8x8x16 slice. The times are simulated.
512 devices in a mesh: member: 2 (over y), gy: 16 (over z), gx: 8 (over x), lev: 2 (over core).
Axes of the slice: x: 8, y: 2, z: 16, core: 2. Of those that a mesh axis runs over, the one named last changes fastest.
The devices are a block of a 8x8x16 slice.
Arguments:
- level_field: bfloat16 [32, 1536, 1536], P(('member', 'lev'), 'gy', 'gx'), parts along dimension 0, may hold values from -6 to 6
Outputs:
- spectra: float32 [1536, 32, 1536], P(('gy', 'gx'), ('member', 'lev')), parts along dimension 1
- spectra_zone: float32 [1536, 32, 11], P(('gy', 'gx'), ('member', 'lev')), parts along dimension 1
There are 2 independent parts, one for each index of `member`. A program takes and returns all parts, laid end to end along the dimension named above; each array names one. Nothing has to cross between parts.
All inputs are finite; a program needn't handle non-finite values.
Results may differ from a plain program's by a relative error of at most 0.0042.
Values may be sent and summed in bfloat16 or wider, within the bound.
No kernel may reach another device: no remote copies, remote signals or barrier semaphores. Data moves between devices by JAX's collectives and lax.ppermute only.
A program may use at most 64 MiB of HBM per device.

v0:
```python
import math

import jax
import jax.numpy as jnp
from jax import lax
from jax.sharding import PartitionSpec as P

NX = 1536
NY = 1536
EXT_ZONE = 11
WAVES = 768


def in_blocks(shard, dim, devices):
    before, after = (shard.shape[:dim], shard.shape[dim + 1 :])
    return jnp.moveaxis(shard.reshape(*before, devices, -1, *after), dim, 0)


def laid_out(blocks, dim):
    dims = list(blocks.shape[1:])
    dims[dim] *= blocks.shape[0]
    return jnp.moveaxis(blocks, 0, dim).reshape(dims)


def joined_exchange(shard, axis, axes, splits, concats):
    sizes = [lax.axis_size(a) for a in axes]
    blocks = in_blocks(shard, splits[0], sizes[0])
    blocks = jnp.moveaxis(in_blocks(blocks, splits[1] + 1, sizes[1]), 0, 1)
    inside = blocks.shape[2:]
    blocks = blocks.reshape(-1, *inside)
    blocks = lax.all_to_all(blocks, axis, split_axis=0, concat_axis=0, tiled=True)
    blocks = laid_out(blocks.reshape(*sizes, *inside), concats[0] + 1)
    return laid_out(blocks, concats[1])


def blend_zone(second_last, last_value, first_value, second_value, zone_count):
    steps = (jnp.arange(zone_count, dtype=jnp.int32) + 1).astype(jnp.float32) / (zone_count + 1.0)
    weight_a = 2.0 * steps**3 - 3.0 * steps**2 + 1.0
    weight_b = steps**3 - 2.0 * steps**2 + steps
    weight_c = -2.0 * steps**3 + 3.0 * steps**2
    weight_d = steps**3 - steps**2
    tangent_scale = zone_count + 1.0
    slope_start = tangent_scale * (last_value - second_last)
    slope_end = tangent_scale * (second_value - first_value)
    return (
        last_value[..., None] * weight_a
        + slope_start[..., None] * weight_b
        + first_value[..., None] * weight_c
        + slope_end[..., None] * weight_d
    )


def make_table(wave_count, length):
    coeff = jnp.arange(2 * wave_count, dtype=jnp.int32)[:, None]
    column = jnp.arange(length, dtype=jnp.int32)[None, :]
    is_cosine = coeff < wave_count
    number = jnp.where(is_cosine, coeff, coeff - wave_count + 1)
    phase = (number * column % length).astype(jnp.float32) * (2.0 * math.pi / length)
    values = jnp.where(is_cosine, jnp.cos(phase), -jnp.sin(phase)) / math.sqrt(length)
    return values.astype(jnp.bfloat16)


def shards(level_field):
    block_count = lax.axis_size("gx")
    band_count = lax.axis_size("gy")
    wave_table = make_table(WAVES, NX + EXT_ZONE)
    core_table = wave_table[:, :NX]
    zone_table = wave_table[:, NX:]
    levels_here = level_field.shape[0]
    wave_share = 2 * WAVES // (band_count * block_count)
    core_rows = lax.all_to_all(level_field, "gx", split_axis=0, concat_axis=2, tiled=True)
    widened = core_rows.astype(jnp.float32)
    zone_cols = blend_zone(
        widened[..., NX - 2], widened[..., NX - 1], widened[..., 0], widened[..., 1], EXT_ZONE
    ).astype(jnp.bfloat16)
    dims = (((1,), (2,)), ((), ()))
    total = lax.dot_general(core_table, core_rows, dims, preferred_element_type=jnp.float32)
    partial_spec = total + lax.dot_general(
        zone_table, zone_cols, dims, preferred_element_type=jnp.float32
    )
    band_rows = partial_spec.shape[2]
    shaped = partial_spec.reshape(
        band_count, block_count, wave_share, 1, levels_here // block_count, 1, band_rows
    )
    moved = joined_exchange(
        shaped.astype(jnp.bfloat16), ("gy", "gx"), ("gy", "gx"), (0, 1), (5, 3)
    ).astype(shaped.dtype)
    spectra = moved.reshape(wave_share, levels_here, NY)
    spectra_zone = blend_zone(
        spectra[..., NY - 2], spectra[..., NY - 1], spectra[..., 0], spectra[..., 1], EXT_ZONE
    )
    return (spectra, spectra_zone)


def solution(mesh):
    return jax.shard_map(
        shards,
        mesh=mesh,
        in_specs=(P(("member", "lev"), "gy", "gx"),),
        out_specs=(
            P(("gy", "gx"), ("member", "lev"), None),
            P(("gy", "gx"), ("member", "lev"), None),
        ),
        check_vma=False,
    )
```

profile of v0, /device:TPU:80, one launch (start us, length us, event | category | flops | bytes accessed | tf_op | source)
XLA Modules:
  0.0 155.7 jit_solution(11122747929397508799)
XLA Ops:
  0.6 7.3 %all-to-all-start = ((bf16[8,96,192]{2,1,0:T(8,128)(2,1)}), bf16[8,96,192]{2,1,0:T(8,128)(2,1)S(1)}, u32[]{:S(2)}, u32[]{:S(2)}) async-start(bf16[8,96,192]{2,1,0:T(8,128)(2,1)} %param.1), calls=%async_computation | async-start | bytes 786432 | tf_op jit(solution)/shard_map/all_to_all | solution.py:71
  8.0 46.7 %multiply_convert_fusion = bf16[1536,1547]{1,0:T(8,128)(2,1)} fusion(s32[1536]{0:T(1024)S(1)} %add_select_fusion.1, pred[1536]{0:T(1024)(128)(4,1)S(1)} %iota_compare_fusion), kind=kLoop, calls=%fused_computation.3 | loop fusion | flops 30890496 | bytes 4760064 | tf_op jit(solution)/shard_map/convert_element_type | solution.py:60
  54.7 0.0 all-to-all-done
  54.7 0.2 copy.21
  55.0 0.3 reshape.171
  55.3 0.1 bitcast_convert_fusion
  55.4 0.5 copy.22
  55.8 0.3 reshape.173
  56.1 0.2 slice_reduce_fusion.1
  56.3 3.9 %fusion.5 = f32[1536,96]{0,1:T(8,128)S(1)} fusion(bf16[96,1536]{1,0:T(8,128)(2,1)S(1)} %reshape.171, bf16[1536,1547]{1,0:T(8,128)(2,1)} %multiply_convert_fusion), kind=kOutput, calls=%fused_computation.8 | convolution fusion | flops 452984832 | bytes 5603328 | tf_op jit(solution)/shard_map/dot_general | solution.py:77
  60.2 1.4 fusion.7
  61.6 0.2 copy.23
  61.8 0.1 convert_element_type.100
  61.9 83.1 %all_to_all.20 = bf16[128,1,1,12,1,1,1,96]{7,3,6,5,4,2,1,0:T(8,128)(2,1)S(1)} all-to-all(bf16[128,1,1,12,1,1,1,96]{7,3,6,5,4,2,1,0:T(8,128)(2,1)S(1)} %bitcast.30), channel_id=1, replica_groups=mesh['member'=2,'gy'=16,'gx'=8,'lev'=2] {'gy','gx'}, dimensions={0} | all-to-all | bytes 589824 | tf_op jit(solution)/shard_map/all_to_all | solution.py:31
  145.0 4.0 %copy.25 = f32[16,8,1,1,12,1,1,1,96]{4,1,8,0,7,6,5,3,2:T(8,128)} copy(bf16[16,8,1,1,12,1,1,1,96]{8,4,1,0,7,6,5,3,2:T(8,128)(2,1)S(1)} %bitcast.31) | data formatting | bytes 884736 | tf_op jit(solution)/shard_map/convert_element_type | solution.py:87
  149.0 0.7 slice_bitcast_fusion.1
  149.7 5.3 %copy.26 = f32[12,8,1536]{2,1,0:T(8,128)} copy(f32[12,8,1536]{0,1,2:T(8,128)} %bitcast.28) | data formatting | bytes 1179648
  155.0 0.7 multiply_add_fusion
  (4 shorter events, 0.0 us)
Async XLA Ops:
  0.6 54.1 %all-to-all-start = ((bf16[8,96,192]{2,1,0:T(8,128)(2,1)}), bf16[8,96,192]{2,1,0:T(8,128)(2,1)S(1)}, u32[]{:S(2)}, u32[]{:S(2)}) async-start(bf16[8,96,192]{2,1,0:T(8,128)(2,1)} %param.1), calls=%async_computation | async-start | bytes 786432 | tf_op jit(solution)/shard_map/all_to_all | solution.py:71
where the time goes:
time: 157 us; the launch traced here: 156 us
  blocking collectives  83.1 us (53%)
  other arithmetic  48.5 us (31%)
  local copies, waits for them, and re-layouts  10.8 us (7%)
  starting transfers between devices  7.33 us (5%)
  matrix products  5.26 us (3%)
    all_to_all x1, blocking collectives, joined_exchange(): lax.all_to_all(blocks, axis, split_axis=0, concat_axis=0, tiled=True)  83.1 us
    convert_element_type x1, other arithmetic, make_table(): return values.astype(jnp.bfloat16)  46.7 us
    all_to_all x1, starting transfers between devices, shards(): lax.all_to_all(level_field, 'gx', split_axis=0, concat_axis=2, tiled=True)  7.33 us
    unnamed x1, local copies, waits for them, and re-layouts  5.28 us
    convert_element_type x1, local copies, waits for them, and re-layouts, shards(): moved = joined_exchange(shaped.astype(jnp.bfloat16), ('gy', 'gx'), ('gy',...  3.95 us
    dot_general x1, matrix products, shards(): lax.dot_general(core_table, core_rows, dims, preferred_element_type=jnp.f...  3.88 us
  transfers between devices with their start and end apart: 1, of which 0 were waited for; matrix products, arithmetic and copies ran while one was open for 30% of the time, Pallas kernels for 0%

commit v1 on v0

v1 whole, which is shorter than its diff:
```python
import functools
import math

import jax
import jax.numpy as jnp
from jax import lax
from jax.experimental import pallas as pl
from jax.experimental.pallas import tpu as pltpu
from jax.sharding import Mesh, PartitionSpec as P

EXT_ZONE = 11
LANES = 128
HALF = LANES // 2
ROWS = 8
UNROLL = 4
INTERPRET = False


def blend(second_last, last_value, first_value, second_value, steps):
    weight_a = 2.0 * steps * steps * steps - 3.0 * steps * steps + 1.0
    weight_b = steps * steps * steps - 2.0 * steps * steps + steps
    weight_c = -2.0 * steps * steps * steps + 3.0 * steps * steps
    weight_d = steps * steps * steps - steps * steps
    scale = EXT_ZONE + 1.0
    slope_start = scale * (last_value - second_last)
    slope_end = scale * (second_value - first_value)
    return last_value * weight_a + slope_start * weight_b + first_value * weight_c + slope_end * weight_d


def sin_cos(turns, length):
    turns = turns - length * jnp.round(turns * (1.0 / length))
    half = turns * (math.pi / length)
    sq = half * half
    s = sq * (-1.0 / 39916800.0) + 1.0 / 362880.0
    s = s * sq - 1.0 / 5040.0
    s = s * sq + 1.0 / 120.0
    s = s * sq - 1.0 / 6.0
    s = (s * sq + 1.0) * half
    c = sq * (1.0 / 479001600.0) - 1.0 / 3628800.0
    c = c * sq + 1.0 / 40320.0
    c = c * sq - 1.0 / 720.0
    c = c * sq + 1.0 / 24.0
    c = c * sq - 0.5
    c = c * sq + 1.0
    return 2.0 * s * c, 1.0 - 2.0 * s * s


def lane_iota(shape):
    return lax.broadcasted_iota(jnp.int32, shape, 1)


def row_iota(shape):
    return lax.broadcasted_iota(jnp.int32, shape, 0)


def turned(p, q, angle):
    s, c = angle
    return p * c - q * s, q * c + p * s


def twice(angle):
    s, c = angle
    return 2.0 * s * c, 1.0 - 2.0 * s * s


def pack_kernel(field_hbm, out_hbm, field_ref, packed_ref, arrived, sent):
    levels, lats, _ = field_ref.shape
    pairs = levels // 2
    copies = out_hbm.shape[0] // pairs

    def fetch(level):
        return pltpu.make_async_copy(field_hbm.at[level], field_ref.at[level], arrived.at[level])

    def send(pair, copy):
        at = copy * pairs + pair
        return pltpu.make_async_copy(packed_ref.at[pair], out_hbm.at[at], sent.at[at])

    for pair in range(pairs):
        fetch(pair).start()
        fetch(pair + pairs).start()
    for pair in range(pairs):
        fetch(pair).wait()
        fetch(pair + pairs).wait()
        near, far = field_ref[pair], field_ref[pair + pairs]
        rest = [v[:, LANES:].astype(jnp.float32) for v in (near, far)]
        packed_ref[pair, :lats, :] = near[:, :LANES]
        packed_ref[pair, lats : 2 * lats, :] = far[:, :LANES]
        packed_ref[pair, 2 * lats :, :] = jnp.concatenate(rest, axis=1).astype(packed_ref.dtype)
        for copy in range(copies):
            send(pair, copy).start()
    for pair in range(pairs):
        for copy in range(copies):
            send(pair, copy).wait()


def table_kernel(half_ref, table_ref, *, bands, blocks, quarter, share, cols):
    length = blocks * cols + EXT_ZONE
    span = share * blocks
    here = share * quarter
    waves = span * bands // 2
    tile = 2 * ROWS
    row = row_iota((tile, LANES))
    lane = lane_iota((tile, LANES))
    lane_f = lane.astype(jnp.float32)
    start = half_ref[0] * here
    scale = 1.0 / math.sqrt(length)
    left = lane < HALF
    per_band = here // tile

    def rows(n, _):
        coeff = start + span * (n // per_band) + tile * (n % per_band) + row
        is_cosine = coeff < waves
        number = jnp.where(is_cosine, coeff, coeff - (waves - 1)).astype(jnp.float32)
        s0, c0 = sin_cos(number * lane_f, float(length))
        by_half = jnp.broadcast_to(s0[:, HALF : HALF + 1], s0.shape), jnp.broadcast_to(c0[:, HALF : HALF + 1], c0.shape)
        s0, c0 = s0 * scale, c0 * scale
        p = jnp.where(is_cosine, c0, -s0)
        q = jnp.where(is_cosine, s0, c0)
        by_lanes = twice(by_half)
        by_block = turned(by_lanes[1], by_lanes[0], by_half)[::-1]
        by_pair = twice(by_block)
        near, far = turned(p, q, by_lanes), turned(p, q, twice(by_lanes))
        p2, q2 = jnp.where(left, near[0], far[0]), jnp.where(left, near[1], far[1])
        firsts = [p, turned(p, q, by_block)[0]]
        step = 2.0 * by_block[1]
        for _ in range(blocks - 1):
            firsts.append(step * firsts[-1] - firsts[-2])
        rests = [p2, turned(p2, q2, by_pair)[0]]
        step = 2.0 * by_pair[1]
        for _ in range(blocks // 2 - 2):
            rests.append(step * rests[-1] - rests[-2])
        at = pl.ds(pl.multiple_of(n * tile, tile), tile)
        for k, value in enumerate(firsts + rests):
            table_ref[at, k * LANES : (k + 1) * LANES] = value.astype(table_ref.dtype)
        return 0

    lax.fori_loop(0, table_ref.shape[0] // tile, rows, 0, unroll=UNROLL)


def transform_kernel(core_ref, table_ref, out_ref, rows_ref, values_ref, wide_ref, *, lats, cols, share):
    blocks = core_ref.shape[0]
    over = cols - LANES
    lane = lane_iota((lats, LANES))
    left = lane < HALF
    for level in range(2):
        lo = level * LANES
        rows_ref[lo + lats : lo + LANES, :] = jnp.zeros((LANES - lats, rows_ref.shape[1]), rows_ref.dtype)
        for b in range(blocks):
            rows_ref[lo : lo + lats, b * LANES : (b + 1) * LANES] = core_ref[b, level * lats : (level + 1) * lats, :]
    first_rest = blocks + 1
    for pair in range(blocks // 2):
        even = core_ref[2 * pair, 2 * lats :, :].astype(jnp.float32)
        odd = core_ref[2 * pair + 1, 2 * lats :, :].astype(jnp.float32)
        merged = (jnp.where(left, even, pltpu.roll(odd, HALF, 1)), jnp.where(left, pltpu.roll(even, HALF, 1), odd))
        at = (first_rest + pair) * LANES
        for level in range(2):
            rows_ref[level * LANES : level * LANES + lats, at : at + LANES] = merged[level].astype(rows_ref.dtype)
    steps = (lane + 1).astype(jnp.float32) / (EXT_ZONE + 1.0)
    last = core_ref[blocks - 1, 2 * lats :, :].astype(jnp.float32)
    for level in range(2):
        head = core_ref[0, level * lats : (level + 1) * lats, :].astype(jnp.float32)
        end = level * HALF + over
        zone = blend(last[:, end - 2 : end - 1], last[:, end - 1 : end], head[:, 0:1], head[:, 1:2], steps)
        zone = jnp.where(lane < EXT_ZONE, zone, 0.0)
        rows_ref[level * LANES : level * LANES + lats, blocks * LANES : first_rest * LANES] = zone.astype(rows_ref.dtype)

    count = values_ref.shape[0]
    size = wide_ref.shape[0]
    piece = LANES - lats
    six = share // 2

    def one(chunk, _):
        at = pl.ds(pl.multiple_of(chunk * count, count), count)
        values_ref[...] = lax.dot_general(
            table_ref[at, :], rows_ref[...], (((1,), (1,)), ((), ())), preferred_element_type=jnp.float32
        )
        for m in range(count // share):
            lo, to = m * share, m * 3 * six
            wide_ref[to : to + share, :] = values_ref[lo : lo + share, :LANES]
            wide_ref[to + share : to + 3 * six, :] = values_ref[lo : lo + six, LANES:]
            rest = values_ref[lo + six : lo + share, LANES:]
            for j in range(3):
                moved = pltpu.roll(rest, lats - piece * j, 1)
                wide_ref[to + six * j : to + six * (j + 1), lats:] = moved[:, lats:]
        out_ref[pl.ds(pl.multiple_of(chunk * size, size), size), :] = wide_ref[...].astype(out_ref.dtype)
        return 0

    lax.fori_loop(0, table_ref.shape[0] // count, one, 0)


def unpack_kernel(in_ref, out_ref, zone_ref, wide_ref, *, lats):
    share, levels, total = out_ref.shape
    pairs = levels // 2
    six = share // 2
    stride = 3 * six
    bands = in_ref.shape[0] // (pairs * stride)
    piece = LANES - lats
    lane = lane_iota((levels, LANES))
    upper = row_iota((levels, LANES)) < pairs
    wide_ref[...] = in_ref[...].astype(jnp.float32)

    def rolled(value, shift):
        return value if shift % LANES == 0 else pltpu.roll(value, shift % LANES, 1)

    def picked(g, at):
        return wide_ref[pl.ds(g * pairs * stride + at, levels, stride=stride), :]

    ends = [jnp.zeros((levels, LANES), jnp.float32) for _ in range(4)]
    for c in range(share):
        first = last = held = None
        fill = 0
        for g in range(0, bands, 2):
            near = picked(g, c)
            if c < six:
                far = picked(g, share + c)
            else:
                parts = [rolled(picked(g, six * j + c - six), piece * j - lats) for j in range(3)]
                far = jnp.where(lane < piece, parts[0], jnp.where(lane < 2 * piece, parts[1], parts[2]))
            both = (
                jnp.where(upper, near, pltpu.roll(far, pairs, 0)),
                jnp.where(upper, pltpu.roll(near, pairs, 0), far),
            )
            for e, value in enumerate(both):
                moved = rolled(value, (g + e) * lats)
                tile = (g + e) * lats // LANES
                current = moved if fill == 0 else jnp.where(lane < fill, held, moved)
                fill += lats
                if fill >= LANES:
                    out_ref[c, :, tile * LANES : (tile + 1) * LANES] = current
                    first = current if tile == 0 else first
                    last = current
                    fill -= LANES
                    held = moved
                else:
                    held = current
        for e, (source, at) in enumerate(((last, LANES - 2), (last, LANES - 1), (first, 0), (first, 1))):
            ends[e] = jnp.where(lane == c, rolled(source, c - at), ends[e])
    for j in range(EXT_ZONE):
        step = jnp.full((levels, LANES), float(j + 1), jnp.float32) / (EXT_ZONE + 1.0)
        zone_ref[j] = blend(*ends, step)[:, :share]


def call(kernel, out_shape, scratch=(), limit=16 << 20, **static):
    return pl.pallas_call(
        functools.partial(kernel, **static),
        out_shape=out_shape,
        scratch_shapes=list(scratch),
        compiler_params=pltpu.CompilerParams(vmem_limit_bytes=limit),
        interpret=INTERPRET,
        name=kernel.__name__,
    )


def shards(level_field):
    halves, quarter = lax.axis_size("gx_half"), lax.axis_size("gx_quarter")
    blocks = halves * quarter
    bands = lax.axis_size("gy")
    levels, lats, cols = level_field.shape
    share = cols // bands
    six = share // 2
    bf16, f32 = jnp.bfloat16, jnp.float32
    assert share * bands == cols and levels == 2 * quarter and halves == 2 and cols == LANES + HALF
    assert share == 2 * six and lats == 3 * (LANES - lats) and bands % 2 == 0 and levels == ROWS

    half = lax.axis_index("gx_half").astype(jnp.int32).reshape(1)
    packed = pl.pallas_call(
        pack_kernel,
        out_shape=jax.ShapeDtypeStruct((blocks, 3 * lats, LANES), bf16),
        in_specs=[pl.BlockSpec(memory_space=pl.ANY)],
        out_specs=pl.BlockSpec(memory_space=pl.ANY),
        scratch_shapes=[
            pltpu.VMEM(level_field.shape, bf16),
            pltpu.VMEM((levels // 2, 3 * lats, LANES), bf16),
            pltpu.SemaphoreType.DMA((levels,)),
            pltpu.SemaphoreType.DMA((blocks,)),
        ],
        compiler_params=pltpu.CompilerParams(vmem_limit_bytes=60 * 1024 * 1024),
        interpret=INTERPRET,
        name="pack_kernel",
    )(level_field)
    core = lax.all_to_all(packed, ("gx_half", "gx_quarter"), split_axis=0, concat_axis=0, tiled=True)
    width = (blocks + 1 + blocks // 2) * LANES
    table = pl.pallas_call(
        functools.partial(table_kernel, bands=bands, blocks=blocks, quarter=quarter, share=share, cols=cols),
        out_shape=jax.ShapeDtypeStruct((share * quarter * bands, width), bf16),
        in_specs=[pl.BlockSpec(memory_space=pltpu.SMEM)],
        compiler_params=pltpu.CompilerParams(vmem_limit_bytes=8 << 20),
        interpret=INTERPRET,
        name="table_kernel",
    )(half)
    dests = bands * quarter
    chunk = dests // 4
    sent = call(
        transform_kernel,
        jax.ShapeDtypeStruct((dests * 3 * six, LANES), bf16),
        scratch=[
            pltpu.VMEM((2 * LANES, width), bf16),
            pltpu.VMEM((chunk * share, 2 * LANES), f32),
            pltpu.VMEM((chunk * 3 * six, LANES), f32),
        ],
        lats=lats,
        cols=cols,
        share=share,
    )(core, table)
    sent = sent.reshape(dests, 3 * six // 2, 2, LANES)
    sent = lax.all_to_all(sent, ("gy", "gx_quarter"), split_axis=0, concat_axis=0, tiled=True)
    sent = sent.reshape(dests * 3 * six, LANES)
    spectra, zone = call(
        unpack_kernel,
        (
            jax.ShapeDtypeStruct((share, levels, lats * bands), f32),
            jax.ShapeDtypeStruct((EXT_ZONE, levels, share), f32),
        ),
        scratch=[pltpu.VMEM((dests * 3 * six, LANES), f32)],
        lats=lats,
    )(sent)
    return spectra, jnp.transpose(zone, (2, 1, 0))


def solution(mesh):
    members, bands, blocks, cores = (mesh.shape[name] for name in ("member", "gy", "gx", "lev"))
    split = Mesh(
        mesh.devices.reshape(members, bands, 2, blocks // 2, cores), ("member", "gy", "gx_half", "gx_quarter", "lev")
    )
    columns = ("gx_half", "gx_quarter")
    coefficients = P(("gy", *columns), ("member", "lev"), None)
    return jax.shard_map(
        shards,
        mesh=split,
        in_specs=(P(("member", "lev"), "gy", columns),),
        out_specs=(coefficients, coefficients),
        check_vma=False,
    )
```

time: 157 us -> 103 us (0.66)
  other arithmetic: 48.5 us -> 0 us
  waiting for transfers between devices: 0.01 us -> 16.5 us
  blocking collectives: 83.1 us -> 67.7 us
  local copies, waits for them, and re-layouts: 10.8 us -> 0 us
  Pallas kernels: 0 us -> 10.4 us
  matrix products: 5.26 us -> 0 us
    convert_element_type x2 -> x0, other arithmetic: 46.8 us -> none  [the longest x1 46.7 us: make_table(): return values.astype(jnp.bfloat16)]
    all_to_all x1, waiting for transfers between devices: 0.01 us -> 16.5 us  [shards(): lax.all_to_all(packed, ('gx_half', 'gx_quarter'), split_axis=0, concat_ax...]
    all_to_all x1, blocking collectives: 83.1 us -> 67.7 us  [shards(): lax.all_to_all(sent, ('gy', 'gx_quarter'), split_axis=0, concat_axis=0, t...]
    pallas_call x0 -> x4, Pallas kernels: none -> 10.4 us  [the longest x1 3.4 us: shards(): call(unpack_kernel, (jax.ShapeDtypeStruct((share, levels, lats * bands),...]
    unnamed x1 -> x0, local copies, waits for them, and re-layouts: 5.28 us -> none
    dot_general x2 -> x0, matrix products: 5.26 us -> none  [the longest x1 3.88 us: shards(): lax.dot_general(core_table, core_rows, dims, preferred_element_type=jnp.f...]
    convert_element_type x5 -> x0, local copies, waits for them, and re-layouts: 5.03 us -> none  [the longest x1 3.95 us: shards(): moved = joined_exchange(shaped.astype(jnp.bfloat16), ('gy', 'gx'), ('gy',...]
  transfers between devices with their start and end apart: 1 -> 1, of which waited for: 0 -> 1; matrix products, arithmetic and copies ran while one was open for 30% -> 0% of each run, Pallas kernels for 0% -> 2%
where the time goes in v1:
time: 103 us
  blocking collectives  67.7 us (66%)
  waiting for transfers between devices  16.5 us (16%)
  Pallas kernels  10.4 us (10%)
  starting transfers between devices  7.33 us (7%)
    all_to_all x1, blocking collectives, shards(): lax.all_to_all(sent, ('gy', 'gx_quarter'), split_axis=0, concat_axis=0, t...  67.7 us
    all_to_all x1, waiting for transfers between devices, shards(): lax.all_to_all(packed, ('gx_half', 'gx_quarter'), split_axis=0, concat_ax...  16.5 us
    all_to_all x1, starting transfers between devices, shards(): lax.all_to_all(packed, ('gx_half', 'gx_quarter'), split_axis=0, concat_ax...  7.33 us
    pallas_call x1, Pallas kernels, shards(): call(unpack_kernel, (jax.ShapeDtypeStruct((share, levels, lats * bands),...  3.4 us
    pallas_call x1, Pallas kernels, shards(): call(transform_kernel, jax.ShapeDtypeStruct((dests * 3 * six, LANES), bf1...  2.57 us
    pallas_call x1, Pallas kernels, shards(): pl.pallas_call(functools.partial(table_kernel, bands=bands, blocks=blocks...  2.48 us
  transfers between devices with their start and end apart: 1, of which 1 were waited for; matrix products, arithmetic and copies ran while one was open for 0% of the time, Pallas kernels for 2%

profile of v1, /device:TPU:80, one launch (start us, length us, event | category | flops | bytes accessed | tf_op | source)
XLA Modules:
  0.0 102.6 jit_solution(4552108663251507565)
XLA Ops:
  0.6 1.9 %pack_kernel.1 = bf16[8,288,128]{2,1,0:T(8,128)(2,1)} custom-call(bf16[8,96,192]{2,1,0:T(8,128)(2,1)} %field_hbm.1), custom_call_target="tpu_custom_call" | custom-call | tf_op jit(solution)/shard_map/pack_kernel/pallas_call | solution.py:266
  2.6 7.3 %all-to-all-start = ((bf16[8,288,128]{2,1,0:T(8,128)(2,1)}), bf16[8,288,128]{2,1,0:T(8,128)(2,1)S(1)}, u32[]{:S(2)}, u32[]{:S(2)}) async-start(bf16[8,288,128]{2,1,0:T(8,128)(2,1)} %pack_kernel.1), calls=%async_computation | async-start | bytes 1179648 | tf_op jit(solution)/shard_map/all_to_all | solution.py:281
  9.9 2.5 %table_kernel.1.table_ref = bf16[768,1664]{1,0:T(8,128)(2,1)S(1)} custom-call(s32[1]{0:T(128)} %bitcast.half_ref), custom_call_target="tpu_custom_call" | custom-call | tf_op jit(solution)/shard_map/table_kernel/pallas_call | solution.py:283
  12.4 16.5 %all-to-all-done.core_ref = bf16[8,288,128]{2,1,0:T(8,128)(2,1)S(1)} async-done(((bf16[8,288,128]{2,1,0:T(8,128)(2,1)}), bf16[8,288,128]{2,1,0:T(8,128)(2,1)S(1)}, u32[]{:S(2)}, u32[]{:S(2)}) %all-to-all-start) | async-done | bytes 589856 | tf_op jit(solution)/shard_map/all_to_all | solution.py:281
  28.9 2.6 %transform_kernel.1 = bf16[1152,128]{1,0:T(8,128)(2,1)S(1)} custom-call(bf16[8,288,128]{2,1,0:T(8,128)(2,1)S(1)} %all-to-all-done.core_ref, bf16[768,1664]{1,0:T(8,128)(2,1)S(1)} %table_kernel.1.table_ref), custom_call_target="tpu_custom_call" | custom-call | tf_op jit(solution)/shard_map/transform_kernel/pallas_call | solution.py:293
  31.5 67.7 %all_to_all.10 = bf16[64,9,2,128]{3,2,1,0:T(2,128)(2,1)S(1)} all-to-all(bf16[64,9,2,128]{3,2,1,0:T(2,128)(2,1)S(1)} %bitcast.5), channel_id=1, replica_groups=mesh['member'=2,'gy'=16,'gx_half'=2,'gx_quarter'=4,'lev'=2] {'gy','gx_qu..., dimensions={0} | all-to-all | bytes 589824 | tf_op jit(solution)/shard_map/all_to_all | solution.py:306
  99.1 3.4 %unpack_kernel.1 = (f32[12,8,1536]{2,1,0:T(8,128)}, f32[11,8,12]{2,1,0:T(8,128)}) custom-call(bf16[1152,128]{1,0:T(8,128)(2,1)S(1)} %bitcast.4), custom_call_target="tpu_custom_call" | custom-call | tf_op jit(solution)/shard_map/unpack_kernel/pallas_call | solution.py:308
Async XLA Ops:
  2.6 26.3 %all-to-all-start = ((bf16[8,288,128]{2,1,0:T(8,128)(2,1)}), bf16[8,288,128]{2,1,0:T(8,128)(2,1)S(1)}, u32[]{:S(2)}, u32[]{:S(2)}) async-start(bf16[8,288,128]{2,1,0:T(8,128)(2,1)} %pack_kernel.1), calls=%async_computation | async-start | bytes 1179648 | tf_op jit(solution)/shard_map/all_to_all | solution.py:281

commit v2 on v0

v2 whole, which is shorter than its diff:
```python
import functools
import math

import jax
import jax.numpy as jnp
from jax import lax
from jax.experimental import pallas as pl
from jax.experimental.pallas import tpu as pltpu
from jax.sharding import PartitionSpec as P

EXT_ZONE = 11
LANES = 128
ROWS = 8
TILE = 2 * ROWS
UNROLL = 4
PACK_UNROLL = 16
INTERPRET = False


def blend(second_last, last_value, first_value, second_value, steps):
    weight_a = 2.0 * steps * steps * steps - 3.0 * steps * steps + 1.0
    weight_b = steps * steps * steps - 2.0 * steps * steps + steps
    weight_c = -2.0 * steps * steps * steps + 3.0 * steps * steps
    weight_d = steps * steps * steps - steps * steps
    scale = EXT_ZONE + 1.0
    slope_start = scale * (last_value - second_last)
    slope_end = scale * (second_value - first_value)
    return last_value * weight_a + slope_start * weight_b + first_value * weight_c + slope_end * weight_d


def sin_cos(turns, length):
    turns = turns - length * jnp.round(turns * (1.0 / length))
    half = turns * (math.pi / length)
    sq = half * half
    s = sq * (-1.0 / 39916800.0) + 1.0 / 362880.0
    s = s * sq - 1.0 / 5040.0
    s = s * sq + 1.0 / 120.0
    s = s * sq - 1.0 / 6.0
    s = (s * sq + 1.0) * half
    c = sq * (1.0 / 479001600.0) - 1.0 / 3628800.0
    c = c * sq + 1.0 / 40320.0
    c = c * sq - 1.0 / 720.0
    c = c * sq + 1.0 / 24.0
    c = c * sq - 0.5
    c = c * sq + 1.0
    return 2.0 * s * c, 1.0 - 2.0 * s * s


def lane_iota(shape):
    return lax.broadcasted_iota(jnp.int32, shape, 1)


def row_iota(shape):
    return lax.broadcasted_iota(jnp.int32, shape, 0)


def turned(at, by):
    c, s = at
    cb, sb = by
    return c * cb - s * sb, s * cb + c * sb


def twice(angle):
    c, s = angle
    return 1.0 - 2.0 * s * s, 2.0 * s * c


def table_kernel(table_ref, *, blocks, cols, chunk):
    length = blocks * cols + EXT_ZONE
    waves = blocks * cols // 2
    lane = lane_iota((TILE, LANES)).astype(jnp.float32)
    row = row_iota((TILE, LANES))
    scale = 1.0 / math.sqrt(length)

    def pairs(number):
        s, c = sin_cos(number * lane, float(length))
        mid = LANES // 2
        by_mid = jnp.broadcast_to(c[:, mid : mid + 1], c.shape), jnp.broadcast_to(s[:, mid : mid + 1], s.shape)
        by_lanes = twice(by_mid)
        by_block = turned(by_lanes, by_mid)
        near = (c * scale, s * scale)
        far = turned(near, by_lanes)
        side = turned(far, by_lanes)
        left = lane < float(mid)
        halves = blocks // 2
        yield halves * LANES, tuple(jnp.where(left, f, e) for f, e in zip(far, side))
        for b in range(halves):
            yield b * LANES, near
            if b >= 2:
                yield (halves + b - 1) * LANES, far
            near, far = turned(near, by_block), turned(far, by_block)

    per = chunk // TILE

    def rows(n, _):
        first = n // per * (2 * chunk) + n % per * TILE
        for lo, (c, s) in pairs((n * TILE + row).astype(jnp.float32)):
            for part, value in enumerate((c, -s)):
                at = pl.ds(pl.multiple_of(first + part * chunk, TILE), TILE)
                table_ref[at, lo : lo + LANES] = value.astype(table_ref.dtype)
        return 0

    lax.fori_loop(0, waves // TILE, rows, 0, unroll=UNROLL)
    for lo, (c, s) in pairs((waves + row % ROWS).astype(jnp.float32)):
        table_ref[2 * waves :, lo : lo + LANES] = jnp.where(row < ROWS, c, -s).astype(table_ref.dtype)


def transform_kernel(core_ref, table_ref, out_ref, rows_ref, turn_ref, values_ref, wide_ref, *, chunk, share, sent):
    blocks, lats, cols = core_ref.shape
    halves = blocks // 2
    length = blocks * cols + EXT_ZONE
    waves = blocks * cols // 2
    over = cols - LANES
    lane = lane_iota((lats, LANES))
    head = core_ref[0, :, :LANES].astype(jnp.float32)
    steps = (lane - over + 1).astype(jnp.float32) / (EXT_ZONE + 1.0)
    for part in range(2):
        lo = part * LANES
        rows_ref[lo + lats : lo + LANES, :] = jnp.zeros((LANES - lats, rows_ref.shape[1]), rows_ref.dtype)

        def place(tile, value):
            rows_ref[lo : lo + lats, tile * LANES : (tile + 1) * LANES] = value.astype(rows_ref.dtype)

        def others(b):
            value = core_ref[part * halves + b, :, LANES:].astype(jnp.float32)
            return jnp.concatenate([value, jnp.zeros((lats, LANES - over), jnp.float32)], axis=1)

        for b in range(halves):
            place(b, core_ref[part * halves + b, :, :LANES])
        place(halves, others(0) + pltpu.roll(others(1), over, 1))
        for b in range(2, halves):
            value = others(b)
            if part == 1 and b == halves - 1:
                zone = blend(value[:, over - 2 : over - 1], value[:, over - 1 : over], head[:, 0:1], head[:, 1:2], steps)
                value = jnp.where((lane >= over) & (lane < over + EXT_ZONE), zone, value)
            place(halves + b - 1, value)

    shift = float(halves * cols)
    s, c = sin_cos(row_iota((chunk, LANES)).astype(jnp.float32) * shift, float(length))
    turn_ref[0], turn_ref[1] = c, s
    step = 2.0 * math.pi * (chunk * halves * cols % length) / length
    step = math.cos(step), math.sin(step)

    def both(at, count, by):
        values = lax.dot_general(
            table_ref[at, :], rows_ref[...], (((1,), (1,)), ((), ())), preferred_element_type=jnp.float32
        )
        cb, sb = by
        c, s = values[: count // 2], values[count // 2 :]
        c_far, s_far = c[:, LANES:], s[:, LANES:]
        return c[:, :LANES] + (cb * c_far + sb * s_far), s[:, :LANES] + (cb * s_far - sb * c_far)

    def one(n, _):
        by = turn_ref[0], turn_ref[1]
        c, s = both(pl.ds(pl.multiple_of(n * (2 * chunk), 2 * chunk), 2 * chunk), 2 * chunk, by)
        values_ref[pl.ds(waves - 1 + n * chunk, chunk), :] = s
        values_ref[pl.ds(pl.multiple_of(n * chunk, chunk), chunk), :] = c
        turn_ref[0], turn_ref[1] = turned(by, step)
        return 0

    lax.fori_loop(0, waves // chunk, one, 0, unroll=2)
    by = turn_ref[0, :ROWS], turn_ref[1, :ROWS]
    values_ref[2 * waves - 1 : 2 * waves - 1 + ROWS, :] = both(slice(2 * waves, 2 * waves + TILE), TILE, by)[1]

    lane = lane_iota((ROWS, LANES))
    piece = LANES - lats
    extra = share - sent
    block = wide_ref.shape[0] * share // (2 * waves)

    def pack(m, _):
        def picked(i):
            return values_ref[pl.ds(m * (ROWS * share) + i, ROWS, stride=share), :]

        tails = [picked(sent + i) for i in range(extra)]
        for i in range(block):
            value = picked(i)
            if i < sent:
                value = jnp.where(lane < lats, value, pltpu.roll(tails[i % extra], lats - piece * (i // extra), 1))
            wide_ref[pl.ds(m * (ROWS * block) + i, ROWS, stride=block), :] = value
        return 0

    lax.fori_loop(0, wide_ref.shape[0] // (ROWS * block), pack, 0, unroll=PACK_UNROLL)
    out_ref[...] = wide_ref[...].astype(out_ref.dtype)


def unpack_kernel(in_ref, out_ref, zone_ref, flat_ref, *, lats, sent):
    share, levels, total = out_ref.shape
    bands = total // lats
    piece = LANES - lats
    extra = share - sent
    block = in_ref.shape[0] // (bands * levels)
    flat_ref[...] = in_ref[...].astype(jnp.float32)
    lane = lane_iota((levels, LANES))

    def rolled(value, shift):
        return value if shift % LANES == 0 else pltpu.roll(value, shift % LANES, 1)

    def picked(g, i):
        return flat_ref[pl.ds(g * levels * block + i, levels, stride=block), :]

    def pieces(c):
        for g in range(bands):
            if c < sent:
                yield picked(g, c), 0, g * lats, lats
            else:
                for j in range(sent // extra):
                    yield picked(g, j * extra + c - sent), lats, g * lats + piece * j, piece

    ends = [jnp.zeros((levels, LANES), jnp.float32) for _ in range(4)]
    for c in range(share):
        first = last = held = None
        for value, lo, lat, size in pieces(c):
            moved = rolled(value, lat - lo)
            fill = lat % LANES
            held = moved if fill == 0 else jnp.where(lane < fill, held, moved)
            if fill + size >= LANES:
                tile = lat // LANES
                out_ref[c, :, tile * LANES : (tile + 1) * LANES] = held
                first = held if tile == 0 else first
                last = held
                held = moved
        for e, (source, at) in enumerate(((last, LANES - 2), (last, LANES - 1), (first, 0), (first, 1))):
            ends[e] = jnp.where(lane == c, rolled(source, c - at), ends[e])
    for j in range(EXT_ZONE):
        step = jnp.full((levels, LANES), float(j + 1), jnp.float32) / (EXT_ZONE + 1.0)
        zone_ref[j] = blend(*ends, step)[:, :share]


def call(kernel, out_shape, scratch=(), limit=16 << 20, **static):
    return pl.pallas_call(
        functools.partial(kernel, **static),
        out_shape=out_shape,
        scratch_shapes=list(scratch),
        compiler_params=pltpu.CompilerParams(vmem_limit_bytes=limit),
        interpret=INTERPRET,
        name=kernel.__name__,
    )


def shards(level_field):
    blocks, bands = lax.axis_size("gx"), lax.axis_size("gy")
    levels, lats, cols = level_field.shape
    share = cols // bands
    coeffs = share * bands * blocks
    piece = LANES - lats
    parts = lats // piece
    sent = share * parts // (parts + 1)
    block = sent + sent % 2
    chunk = coeffs // 4
    bf16, f32 = jnp.bfloat16, jnp.float32
    assert share * bands == cols and levels == blocks == ROWS and lats == parts * piece
    assert sent * (parts + 1) == share * parts and cols == LANES + LANES // 2 and chunk % TILE == 0

    core = lax.all_to_all(level_field, "gx", split_axis=0, concat_axis=0, tiled=True)
    width = LANES * (blocks - 1)
    table = call(
        table_kernel,
        jax.ShapeDtypeStruct((coeffs + TILE, width), bf16),
        limit=8 << 20,
        blocks=blocks,
        cols=cols,
        chunk=chunk,
    )()
    dests = bands * blocks
    packed = call(
        transform_kernel,
        jax.ShapeDtypeStruct((dests * block, LANES), bf16),
        scratch=[
            pltpu.VMEM((2 * LANES, width), bf16),
            pltpu.VMEM((2, chunk, LANES), f32),
            pltpu.VMEM((coeffs + TILE, LANES), f32),
            pltpu.VMEM((dests * block, LANES), f32),
        ],
        chunk=chunk,
        share=share,
        sent=sent,
    )(core, table)
    packed = packed.reshape(dests, block // 2, 2, LANES)
    packed = lax.all_to_all(packed, ("gy", "gx"), split_axis=0, concat_axis=0, tiled=True)
    packed = packed.reshape(dests * block, LANES)
    spectra, zone = call(
        unpack_kernel,
        (
            jax.ShapeDtypeStruct((share, levels, lats * bands), f32),
            jax.ShapeDtypeStruct((EXT_ZONE, levels, share), f32),
        ),
        scratch=[pltpu.VMEM((dests * block, LANES), f32)],
        lats=lats,
        sent=sent,
    )(packed)
    return spectra, jnp.transpose(zone, (2, 1, 0))


def solution(mesh):
    coefficients = P(("gy", "gx"), ("member", "lev"), None)
    return jax.shard_map(
        shards,
        mesh=mesh,
        in_specs=(P(("member", "lev"), "gy", "gx"),),
        out_specs=(coefficients, coefficients),
        check_vma=False,
    )
```

time: 157 us -> 96 us (0.61)
  other arithmetic: 48.5 us -> 0 us
  blocking collectives: 83.1 us -> 70.1 us
  waiting for transfers between devices: 0.01 us -> 12.4 us
  local copies, waits for them, and re-layouts: 10.8 us -> 0 us
  matrix products: 5.26 us -> 0 us
  Pallas kernels: 0 us -> 5.11 us
    convert_element_type x2 -> x0, other arithmetic: 46.8 us -> none  [the longest x1 46.7 us: make_table(): return values.astype(jnp.bfloat16)]
    all_to_all x1, blocking collectives: 83.1 us -> 70.1 us  [shards(): lax.all_to_all(packed, ('gy', 'gx'), split_axis=0, concat_axis=0, tiled=T...]
    all_to_all x1, waiting for transfers between devices: 0.01 us -> 12.4 us  [shards(): lax.all_to_all(level_field, 'gx', split_axis=0, concat_axis=0, tiled=True)]
    unnamed x1 -> x0, local copies, waits for them, and re-layouts: 5.28 us -> none
    dot_general x2 -> x0, matrix products: 5.26 us -> none  [the longest x1 3.88 us: shards(): lax.dot_general(core_table, core_rows, dims, preferred_element_type=jnp.f...]
    pallas_call x0 -> x3, Pallas kernels: none -> 5.11 us  [the longest x1 2.33 us: shards(): call(table_kernel, jax.ShapeDtypeStruct((coeffs + TILE, width), bf16), li...]
    convert_element_type x5 -> x0, local copies, waits for them, and re-layouts: 5.03 us -> none  [the longest x1 3.95 us: shards(): moved = joined_exchange(shaped.astype(jnp.bfloat16), ('gy', 'gx'), ('gy',...]
  transfers between devices with their start and end apart: 1 -> 1, of which waited for: 0 -> 1; matrix products, arithmetic and copies ran while one was open for 30% -> 0% of each run, Pallas kernels for 0% -> 2%
where the time goes in v2:
time: 96 us; the launch traced here: 95.6 us
  blocking collectives  70.1 us (73%)
  waiting for transfers between devices  12.4 us (13%)
  starting transfers between devices  7.33 us (8%)
  Pallas kernels  5.11 us (5%)
    all_to_all x1, blocking collectives, shards(): lax.all_to_all(packed, ('gy', 'gx'), split_axis=0, concat_axis=0, tiled=T...  70.1 us
    all_to_all x1, waiting for transfers between devices, shards(): lax.all_to_all(level_field, 'gx', split_axis=0, concat_axis=0, tiled=True)  12.4 us
    all_to_all x1, starting transfers between devices, shards(): lax.all_to_all(level_field, 'gx', split_axis=0, concat_axis=0, tiled=True)  7.33 us
    pallas_call x1, Pallas kernels, shards(): call(table_kernel, jax.ShapeDtypeStruct((coeffs + TILE, width), bf16), li...  2.33 us
  transfers between devices with their start and end apart: 1, of which 1 were waited for; matrix products, arithmetic and copies ran while one was open for 0% of the time, Pallas kernels for 2%

profile of v2, /device:TPU:80, one launch (start us, length us, event | category | flops | bytes accessed | tf_op | source)
XLA Modules:
  0.0 95.6 jit_solution(1472503036372571395)
XLA Ops:
  0.6 7.3 %all-to-all-start = ((bf16[8,96,192]{2,1,0:T(8,128)(2,1)}), bf16[8,96,192]{2,1,0:T(8,128)(2,1)S(1)}, u32[]{:S(2)}, u32[]{:S(2)}) async-start(bf16[8,96,192]{2,1,0:T(8,128)(2,1)} %param.1), calls=%async_computation | async-start | bytes 786432 | tf_op jit(solution)/shard_map/all_to_all | solution.py:254
  8.0 2.3 %table_kernel.1.table_ref = bf16[1552,896]{1,0:T(8,128)(2,1)S(1)} custom-call(), custom_call_target="tpu_custom_call" | custom-call | tf_op jit(solution)/shard_map/table_kernel/pallas_call | solution.py:256
  10.3 12.4 %all-to-all-done.core_ref = bf16[8,96,192]{2,1,0:T(8,128)(2,1)S(1)} async-done(((bf16[8,96,192]{2,1,0:T(8,128)(2,1)}), bf16[8,96,192]{2,1,0:T(8,128)(2,1)S(1)}, u32[]{:S(2)}, u32[]{:S(2)}) %all-to-all-start) | async-done | bytes 294944 | tf_op jit(solution)/shard_map/all_to_all | solution.py:254
  22.7 1.4 %transform_kernel.1 = bf16[1280,128]{1,0:T(8,128)(2,1)S(1)} custom-call(bf16[8,96,192]{2,1,0:T(8,128)(2,1)S(1)} %all-to-all-done.core_ref, bf16[1552,896]{1,0:T(8,128)(2,1)S(1)} %table_kernel.1.table_ref), custom_call_target="tpu_custom_call" | custom-call | tf_op jit(solution)/shard_map/transform_kernel/pallas_call | solution.py:265
  24.1 70.1 %all_to_all.10 = bf16[128,5,2,128]{3,2,1,0:T(2,128)(2,1)S(1)} all-to-all(bf16[128,5,2,128]{3,2,1,0:T(2,128)(2,1)S(1)} %bitcast.4), channel_id=1, replica_groups=mesh['member'=2,'gy'=16,'gx'=8,'lev'=2] {'gy','gx'}, dimensions={0} | all-to-all | bytes 655360 | tf_op jit(solution)/shard_map/all_to_all | solution.py:279
  94.2 1.4 %unpack_kernel.1 = (f32[12,8,1536]{2,1,0:T(8,128)}, f32[11,8,12]{2,1,0:T(8,128)}) custom-call(bf16[1280,128]{1,0:T(8,128)(2,1)S(1)} %bitcast.3), custom_call_target="tpu_custom_call" | custom-call | tf_op jit(solution)/shard_map/unpack_kernel/pallas_call | solution.py:281
Async XLA Ops:
  0.6 22.1 %all-to-all-start = ((bf16[8,96,192]{2,1,0:T(8,128)(2,1)}), bf16[8,96,192]{2,1,0:T(8,128)(2,1)S(1)}, u32[]{:S(2)}, u32[]{:S(2)}) async-start(bf16[8,96,192]{2,1,0:T(8,128)(2,1)} %param.1), calls=%async_computation | async-start | bytes 786432 | tf_op jit(solution)/shard_map/all_to_all | solution.py:254

commit v3 on v2

--- a/solution.py
+++ b/solution.py
@@ -14,6 +14,7 @@
 TILE = 2 * ROWS
 UNROLL = 4
 PACK_UNROLL = 16
+BAND_STEP = 13
 INTERPRET = False
 
 
@@ -166,10 +167,12 @@
     piece = LANES - lats
     extra = share - sent
     block = wide_ref.shape[0] * share // (2 * waves)
+    bands = wide_ref.shape[0] // (ROWS * block)
 
     def pack(m, _):
         def picked(i):
-            return values_ref[pl.ds(m * (ROWS * share) + i, ROWS, stride=share), :]
+            band = lax.rem(m * BAND_STEP, bands)
+            return values_ref[pl.ds(band * (ROWS * share) + i, ROWS, stride=share), :]
 
         tails = [picked(sent + i) for i in range(extra)]
         for i in range(block):
@@ -179,11 +182,11 @@
             wide_ref[pl.ds(m * (ROWS * block) + i, ROWS, stride=block), :] = value
         return 0
 
-    lax.fori_loop(0, wide_ref.shape[0] // (ROWS * block), pack, 0, unroll=PACK_UNROLL)
+    lax.fori_loop(0, bands, pack, 0, unroll=PACK_UNROLL)
     out_ref[...] = wide_ref[...].astype(out_ref.dtype)
 
 
-def unpack_kernel(in_ref, out_ref, zone_ref, flat_ref, *, lats, sent):
+def unpack_kernel(in_ref, out_hbm, zone_ref, flat_ref, out_ref, leaving, *, lats, sent):
     share, levels, total = out_ref.shape
     bands = total // lats
     piece = LANES - lats
@@ -200,11 +203,15 @@
 
     def pieces(c):
         for g in range(bands):
+            at = next(m for m in range(bands) if m * BAND_STEP % bands == g)
             if c < sent:
-                yield picked(g, c), 0, g * lats, lats
+                yield picked(at, c), 0, g * lats, lats
             else:
                 for j in range(sent // extra):
-                    yield picked(g, j * extra + c - sent), lats, g * lats + piece * j, piece
+                    yield picked(at, j * extra + c - sent), lats, g * lats + piece * j, piece
+
+    def send(c):
+        return pltpu.make_async_copy(out_ref.at[c], out_hbm.at[c], leaving.at[c])
 
     ends = [jnp.zeros((levels, LANES), jnp.float32) for _ in range(4)]
     for c in range(share):
@@ -219,11 +226,14 @@
                 first = held if tile == 0 else first
                 last = held
                 held = moved
+        send(c).start()
         for e, (source, at) in enumerate(((last, LANES - 2), (last, LANES - 1), (first, 0), (first, 1))):
             ends[e] = jnp.where(lane == c, rolled(source, c - at), ends[e])
     for j in range(EXT_ZONE):
         step = jnp.full((levels, LANES), float(j + 1), jnp.float32) / (EXT_ZONE + 1.0)
         zone_ref[j] = blend(*ends, step)[:, :share]
+    for c in range(share):
+        send(c).wait()
 
 
 def call(kernel, out_shape, scratch=(), limit=16 << 20, **static):
@@ -248,7 +258,7 @@
     block = sent + sent % 2
     chunk = coeffs // 4
     bf16, f32 = jnp.bfloat16, jnp.float32
-    assert share * bands == cols and levels == blocks == ROWS and lats == parts * piece
+    assert share * bands == cols and math.gcd(bands, BAND_STEP) == 1 and levels == blocks == ROWS and lats == parts * piece
     assert sent * (parts + 1) == share * parts and cols == LANES + LANES // 2 and chunk % TILE == 0
 
     core = lax.all_to_all(level_field, "gx", split_axis=0, concat_axis=0, tiled=True)
@@ -276,17 +286,26 @@
         sent=sent,
     )(core, table)
     packed = packed.reshape(dests, block // 2, 2, LANES)
-    packed = lax.all_to_all(packed, ("gy", "gx"), split_axis=0, concat_axis=0, tiled=True)
+    order = [m * BAND_STEP % bands * blocks + x for m in range(bands) for x in range(blocks)]
+    packed = lax.all_to_all(
+        packed, ("gy", "gx"), split_axis=0, concat_axis=0, tiled=True, axis_index_groups=[order]
+    )
     packed = packed.reshape(dests * block, LANES)
-    spectra, zone = call(
-        unpack_kernel,
-        (
+    spectra, zone = pl.pallas_call(
+        functools.partial(unpack_kernel, lats=lats, sent=sent),
+        out_shape=(
             jax.ShapeDtypeStruct((share, levels, lats * bands), f32),
             jax.ShapeDtypeStruct((EXT_ZONE, levels, share), f32),
         ),
-        scratch=[pltpu.VMEM((dests * block, LANES), f32)],
-        lats=lats,
-        sent=sent,
+        out_specs=(pl.BlockSpec(memory_space=pl.ANY), pl.BlockSpec(memory_space=pltpu.VMEM)),
+        scratch_shapes=[
+            pltpu.VMEM((dests * block, LANES), f32),
+            pltpu.VMEM((share, levels, lats * bands), f32),
+            pltpu.SemaphoreType.DMA((share,)),
+        ],
+        compiler_params=pltpu.CompilerParams(vmem_limit_bytes=16 << 20),
+        interpret=INTERPRET,
+        name="unpack_kernel",
     )(packed)
     return spectra, jnp.transpose(zone, (2, 1, 0))
 

time: 96 us -> 95.7 us (level); the launches traced: 95.6 us -> 93.8 us
  blocking collectives: 70.1 us -> 67.8 us
    all_to_all x1, blocking collectives: 70.1 us -> 67.8 us  [shards(): lax.all_to_all(packed, ('gy', 'gx'), split_axis=0, concat_axis=0, tiled=T...]
where the time goes in v3:
time: 95.7 us; the launch traced here: 93.8 us
  blocking collectives  67.8 us (71%)
  waiting for transfers between devices  12.4 us (13%)
  starting transfers between devices  7.33 us (8%)
  Pallas kernels  5.64 us (6%)
    all_to_all x1, blocking collectives, shards(): lax.all_to_all(packed, ('gy', 'gx'), split_axis=0, concat_axis=0, tiled=T...  67.8 us
    all_to_all x1, waiting for transfers between devices, shards(): lax.all_to_all(level_field, 'gx', split_axis=0, concat_axis=0, tiled=True)  12.4 us
    all_to_all x1, starting transfers between devices, shards(): lax.all_to_all(level_field, 'gx', split_axis=0, concat_axis=0, tiled=True)  7.33 us
    pallas_call x1, Pallas kernels, shards(): call(table_kernel, jax.ShapeDtypeStruct((coeffs + TILE, width), bf16), li...  2.33 us
  transfers between devices with their start and end apart: 1, of which 1 were waited for; matrix products, arithmetic and copies ran while one was open for 0% of the time, Pallas kernels for 2%

profile of v3, /device:TPU:80, one launch (start us, length us, event | category | flops | bytes accessed | tf_op | source)
XLA Modules:
  0.0 93.8 jit_solution(15063167390262631218)
XLA Ops:
  0.6 7.3 %all-to-all-start = ((bf16[8,96,192]{2,1,0:T(8,128)(2,1)}), bf16[8,96,192]{2,1,0:T(8,128)(2,1)S(1)}, u32[]{:S(2)}, u32[]{:S(2)}) async-start(bf16[8,96,192]{2,1,0:T(8,128)(2,1)} %param.1), calls=%async_computation | async-start | bytes 786432 | tf_op jit(solution)/shard_map/all_to_all | solution.py:264
  8.0 2.3 %table_kernel.1.table_ref = bf16[1552,896]{1,0:T(8,128)(2,1)S(1)} custom-call(), custom_call_target="tpu_custom_call" | custom-call | tf_op jit(solution)/shard_map/table_kernel/pallas_call | solution.py:266
  10.3 12.4 %all-to-all-done.core_ref = bf16[8,96,192]{2,1,0:T(8,128)(2,1)S(1)} async-done(((bf16[8,96,192]{2,1,0:T(8,128)(2,1)}), bf16[8,96,192]{2,1,0:T(8,128)(2,1)S(1)}, u32[]{:S(2)}, u32[]{:S(2)}) %all-to-all-start) | async-done | bytes 294944 | tf_op jit(solution)/shard_map/all_to_all | solution.py:264
  22.7 1.4 %transform_kernel.1 = bf16[1280,128]{1,0:T(8,128)(2,1)S(1)} custom-call(bf16[8,96,192]{2,1,0:T(8,128)(2,1)S(1)} %all-to-all-done.core_ref, bf16[1552,896]{1,0:T(8,128)(2,1)S(1)} %table_kernel.1.table_ref), custom_call_target="tpu_custom_call" | custom-call | tf_op jit(solution)/shard_map/transform_kernel/pallas_call | solution.py:275
  24.1 67.8 %all_to_all.10 = bf16[128,5,2,128]{3,2,1,0:T(2,128)(2,1)S(1)} all-to-all(bf16[128,5,2,128]{3,2,1,0:T(2,128)(2,1)S(1)} %bitcast.4), channel_id=1, replica_groups={{0,2,4,6,8,10,12,14,208,210,212,214,216,218,220,222,160,162,164,166,168..., dimensions={0} | all-to-all | bytes 655360 | tf_op jit(solution)/shard_map/all_to_all | solution.py:290
  91.9 1.9 %unpack_kernel.1 = (f32[12,8,1536]{2,1,0:T(8,128)}, f32[11,8,12]{2,1,0:T(8,128)}) custom-call(bf16[1280,128]{1,0:T(8,128)(2,1)S(1)} %bitcast.3), custom_call_target="tpu_custom_call" | custom-call | tf_op jit(solution)/shard_map/unpack_kernel/pallas_call | solution.py:294
Async XLA Ops:
  0.6 22.1 %all-to-all-start = ((bf16[8,96,192]{2,1,0:T(8,128)(2,1)}), bf16[8,96,192]{2,1,0:T(8,128)(2,1)S(1)}, u32[]{:S(2)}, u32[]{:S(2)}) async-start(bf16[8,96,192]{2,1,0:T(8,128)(2,1)} %param.1), calls=%async_computation | async-start | bytes 786432 | tf_op jit(solution)/shard_map/all_to_all | solution.py:264

commit v4 on v2

--- a/solution.py
+++ b/solution.py
@@ -14,6 +14,7 @@
 TILE = 2 * ROWS
 UNROLL = 4
 PACK_UNROLL = 16
+BAND_STEP = 13
 INTERPRET = False
 
 
@@ -166,10 +167,12 @@
     piece = LANES - lats
     extra = share - sent
     block = wide_ref.shape[0] * share // (2 * waves)
+    bands = wide_ref.shape[0] // (ROWS * block)
 
     def pack(m, _):
         def picked(i):
-            return values_ref[pl.ds(m * (ROWS * share) + i, ROWS, stride=share), :]
+            band = lax.rem(m * BAND_STEP, bands)
+            return values_ref[pl.ds(band * (ROWS * share) + i, ROWS, stride=share), :]
 
         tails = [picked(sent + i) for i in range(extra)]
         for i in range(block):
@@ -179,7 +182,7 @@
             wide_ref[pl.ds(m * (ROWS * block) + i, ROWS, stride=block), :] = value
         return 0
 
-    lax.fori_loop(0, wide_ref.shape[0] // (ROWS * block), pack, 0, unroll=PACK_UNROLL)
+    lax.fori_loop(0, bands, pack, 0, unroll=PACK_UNROLL)
     out_ref[...] = wide_ref[...].astype(out_ref.dtype)
 
 
@@ -200,11 +203,12 @@
 
     def pieces(c):
         for g in range(bands):
+            at = next(m for m in range(bands) if m * BAND_STEP % bands == g)
             if c < sent:
-                yield picked(g, c), 0, g * lats, lats
+                yield picked(at, c), 0, g * lats, lats
             else:
                 for j in range(sent // extra):
-                    yield picked(g, j * extra + c - sent), lats, g * lats + piece * j, piece
+                    yield picked(at, j * extra + c - sent), lats, g * lats + piece * j, piece
 
     ends = [jnp.zeros((levels, LANES), jnp.float32) for _ in range(4)]
     for c in range(share):
@@ -248,7 +252,7 @@
     block = sent + sent % 2
     chunk = coeffs // 4
     bf16, f32 = jnp.bfloat16, jnp.float32
-    assert share * bands == cols and levels == blocks == ROWS and lats == parts * piece
+    assert share * bands == cols and math.gcd(bands, BAND_STEP) == 1 and levels == blocks == ROWS and lats == parts * piece
     assert sent * (parts + 1) == share * parts and cols == LANES + LANES // 2 and chunk % TILE == 0
 
     core = lax.all_to_all(level_field, "gx", split_axis=0, concat_axis=0, tiled=True)
@@ -276,7 +280,10 @@
         sent=sent,
     )(core, table)
     packed = packed.reshape(dests, block // 2, 2, LANES)
-    packed = lax.all_to_all(packed, ("gy", "gx"), split_axis=0, concat_axis=0, tiled=True)
+    order = [m * BAND_STEP % bands * blocks + x for m in range(bands) for x in range(blocks)]
+    packed = lax.all_to_all(
+        packed, ("gy", "gx"), split_axis=0, concat_axis=0, tiled=True, axis_index_groups=[order]
+    )
     packed = packed.reshape(dests * block, LANES)
     spectra, zone = call(
         unpack_kernel,

time: 96 us -> 95.1 us (level); the launches traced: 95.6 us -> 93.3 us
  blocking collectives: 70.1 us -> 67.8 us
    all_to_all x1, blocking collectives: 70.1 us -> 67.8 us  [shards(): lax.all_to_all(packed, ('gy', 'gx'), split_axis=0, concat_axis=0, tiled=T...]
  transfers between devices with their start and end apart: 1 -> 1, of which waited for: 1 -> 1; matrix products, arithmetic and copies ran while one was open for 0% -> 0% of each run, Pallas kernels for 2% -> 3%
where the time goes in v4:
time: 95.1 us; the launch traced here: 93.3 us
  blocking collectives  67.8 us (71%)
  waiting for transfers between devices  12.4 us (13%)
  starting transfers between devices  7.33 us (8%)
  Pallas kernels  5.12 us (5%)
    all_to_all x1, blocking collectives, shards(): lax.all_to_all(packed, ('gy', 'gx'), split_axis=0, concat_axis=0, tiled=T...  67.8 us
    all_to_all x1, waiting for transfers between devices, shards(): lax.all_to_all(level_field, 'gx', split_axis=0, concat_axis=0, tiled=True)  12.4 us
    all_to_all x1, starting transfers between devices, shards(): lax.all_to_all(level_field, 'gx', split_axis=0, concat_axis=0, tiled=True)  7.33 us
    pallas_call x1, Pallas kernels, shards(): call(table_kernel, jax.ShapeDtypeStruct((coeffs + TILE, width), bf16), li...  2.33 us
  transfers between devices with their start and end apart: 1, of which 1 were waited for; matrix products, arithmetic and copies ran while one was open for 0% of the time, Pallas kernels for 3%

profile of v4, /device:TPU:80, one launch (start us, length us, event | category | flops | bytes accessed | tf_op | source)
XLA Modules:
  0.0 93.3 jit_solution(14666513837626504348)
XLA Ops:
  0.6 7.3 %all-to-all-start = ((bf16[8,96,192]{2,1,0:T(8,128)(2,1)}), bf16[8,96,192]{2,1,0:T(8,128)(2,1)S(1)}, u32[]{:S(2)}, u32[]{:S(2)}) async-start(bf16[8,96,192]{2,1,0:T(8,128)(2,1)} %param.1), calls=%async_computation | async-start | bytes 786432 | tf_op jit(solution)/shard_map/all_to_all | solution.py:258
  8.0 2.3 %table_kernel.1.table_ref = bf16[1552,896]{1,0:T(8,128)(2,1)S(1)} custom-call(), custom_call_target="tpu_custom_call" | custom-call | tf_op jit(solution)/shard_map/table_kernel/pallas_call | solution.py:260
  10.3 12.4 %all-to-all-done.core_ref = bf16[8,96,192]{2,1,0:T(8,128)(2,1)S(1)} async-done(((bf16[8,96,192]{2,1,0:T(8,128)(2,1)}), bf16[8,96,192]{2,1,0:T(8,128)(2,1)S(1)}, u32[]{:S(2)}, u32[]{:S(2)}) %all-to-all-start) | async-done | bytes 294944 | tf_op jit(solution)/shard_map/all_to_all | solution.py:258
  22.7 1.4 %transform_kernel.1 = bf16[1280,128]{1,0:T(8,128)(2,1)S(1)} custom-call(bf16[8,96,192]{2,1,0:T(8,128)(2,1)S(1)} %all-to-all-done.core_ref, bf16[1552,896]{1,0:T(8,128)(2,1)S(1)} %table_kernel.1.table_ref), custom_call_target="tpu_custom_call" | custom-call | tf_op jit(solution)/shard_map/transform_kernel/pallas_call | solution.py:269
  24.1 67.8 %all_to_all.10 = bf16[128,5,2,128]{3,2,1,0:T(2,128)(2,1)S(1)} all-to-all(bf16[128,5,2,128]{3,2,1,0:T(2,128)(2,1)S(1)} %bitcast.4), channel_id=1, replica_groups={{0,2,4,6,8,10,12,14,208,210,212,214,216,218,220,222,160,162,164,166,168..., dimensions={0} | all-to-all | bytes 655360 | tf_op jit(solution)/shard_map/all_to_all | solution.py:284
  91.9 1.4 %unpack_kernel.1 = (f32[12,8,1536]{2,1,0:T(8,128)}, f32[11,8,12]{2,1,0:T(8,128)}) custom-call(bf16[1280,128]{1,0:T(8,128)(2,1)S(1)} %bitcast.3), custom_call_target="tpu_custom_call" | custom-call | tf_op jit(solution)/shard_map/unpack_kernel/pallas_call | solution.py:288
Async XLA Ops:
  0.6 22.1 %all-to-all-start = ((bf16[8,96,192]{2,1,0:T(8,128)(2,1)}), bf16[8,96,192]{2,1,0:T(8,128)(2,1)S(1)}, u32[]{:S(2)}, u32[]{:S(2)}) async-start(bf16[8,96,192]{2,1,0:T(8,128)(2,1)} %param.1), calls=%async_computation | async-start | bytes 786432 | tf_op jit(solution)/shard_map/all_to_all | solution.py:258

commit v5 on v4

--- a/solution.py
+++ b/solution.py
@@ -201,30 +201,28 @@
     def picked(g, i):
         return flat_ref[pl.ds(g * levels * block + i, levels, stride=block), :]
 
-    def pieces(c):
+    ends = [jnp.zeros((levels, LANES), jnp.float32) for _ in range(4)]
+    held = [None] * share
+
+    def place(c, value, lo, lat, size):
+        moved = rolled(value, lat - lo)
+        fill = lat % LANES
+        held[c] = moved if fill == 0 else jnp.where(lane < fill, held[c], moved)
+        if fill + size >= LANES:
+            tile = lat // LANES
+            out_ref[c, :, tile * LANES : (tile + 1) * LANES] = held[c]
+            for e, (edge, at) in enumerate(((total // LANES - 1, LANES - 2), (total // LANES - 1, LANES - 1), (0, 0), (0, 1))):
+                if tile == edge:
+                    ends[e] = jnp.where(lane == c, rolled(held[c], c - at), ends[e])
+            held[c] = moved
+
+    for i in range(extra):
         for g in range(bands):
             at = next(m for m in range(bands) if m * BAND_STEP % bands == g)
-            if c < sent:
-                yield picked(at, c), 0, g * lats, lats
-            else:
-                for j in range(sent // extra):
-                    yield picked(at, j * extra + c - sent), lats, g * lats + piece * j, piece
-
-    ends = [jnp.zeros((levels, LANES), jnp.float32) for _ in range(4)]
-    for c in range(share):
-        first = last = held = None
-        for value, lo, lat, size in pieces(c):
-            moved = rolled(value, lat - lo)
-            fill = lat % LANES
-            held = moved if fill == 0 else jnp.where(lane < fill, held, moved)
-            if fill + size >= LANES:
-                tile = lat // LANES
-                out_ref[c, :, tile * LANES : (tile + 1) * LANES] = held
-                first = held if tile == 0 else first
-                last = held
-                held = moved
-        for e, (source, at) in enumerate(((last, LANES - 2), (last, LANES - 1), (first, 0), (first, 1))):
-            ends[e] = jnp.where(lane == c, rolled(source, c - at), ends[e])
+            for j in range(sent // extra):
+                value = picked(at, j * extra + i)
+                place(j * extra + i, value, 0, g * lats, lats)
+                place(sent + i, value, lats, g * lats + piece * j, piece)
     for j in range(EXT_ZONE):
         step = jnp.full((levels, LANES), float(j + 1), jnp.float32) / (EXT_ZONE + 1.0)
         zone_ref[j] = blend(*ends, step)[:, :share]

time: 95.1 us -> 95.2 us (level)
  transfers between devices with their start and end apart: 1 -> 1, of which waited for: 1 -> 1; matrix products, arithmetic and copies ran while one was open for 0% -> 0% of each run, Pallas kernels for 3% -> 2%
where the time goes in v5:
time: 95.2 us; the launch traced here: 93.4 us
  blocking collectives  67.8 us (71%)
  waiting for transfers between devices  12.4 us (13%)
  starting transfers between devices  7.33 us (8%)
  Pallas kernels  5.2 us (5%)
    all_to_all x1, blocking collectives, shards(): lax.all_to_all(packed, ('gy', 'gx'), split_axis=0, concat_axis=0, tiled=T...  67.8 us
    all_to_all x1, waiting for transfers between devices, shards(): lax.all_to_all(level_field, 'gx', split_axis=0, concat_axis=0, tiled=True)  12.4 us
    all_to_all x1, starting transfers between devices, shards(): lax.all_to_all(level_field, 'gx', split_axis=0, concat_axis=0, tiled=True)  7.33 us
    pallas_call x1, Pallas kernels, shards(): call(table_kernel, jax.ShapeDtypeStruct((coeffs + TILE, width), bf16), li...  2.33 us
  transfers between devices with their start and end apart: 1, of which 1 were waited for; matrix products, arithmetic and copies ran while one was open for 0% of the time, Pallas kernels for 2%

profile of v5, /device:TPU:80, one launch (start us, length us, event | category | flops | bytes accessed | tf_op | source)
XLA Modules:
  0.0 93.4 jit_solution(1538538840873919637)
XLA Ops:
  0.6 7.3 %all-to-all-start = ((bf16[8,96,192]{2,1,0:T(8,128)(2,1)}), bf16[8,96,192]{2,1,0:T(8,128)(2,1)S(1)}, u32[]{:S(2)}, u32[]{:S(2)}) async-start(bf16[8,96,192]{2,1,0:T(8,128)(2,1)} %param.1), calls=%async_computation | async-start | bytes 786432 | tf_op jit(solution)/shard_map/all_to_all | solution.py:256
  8.0 2.3 %table_kernel.1.table_ref = bf16[1552,896]{1,0:T(8,128)(2,1)S(1)} custom-call(), custom_call_target="tpu_custom_call" | custom-call | tf_op jit(solution)/shard_map/table_kernel/pallas_call | solution.py:258
  10.3 12.4 %all-to-all-done.core_ref = bf16[8,96,192]{2,1,0:T(8,128)(2,1)S(1)} async-done(((bf16[8,96,192]{2,1,0:T(8,128)(2,1)}), bf16[8,96,192]{2,1,0:T(8,128)(2,1)S(1)}, u32[]{:S(2)}, u32[]{:S(2)}) %all-to-all-start) | async-done | bytes 294944 | tf_op jit(solution)/shard_map/all_to_all | solution.py:256
  22.7 1.4 %transform_kernel.1 = bf16[1280,128]{1,0:T(8,128)(2,1)S(1)} custom-call(bf16[8,96,192]{2,1,0:T(8,128)(2,1)S(1)} %all-to-all-done.core_ref, bf16[1552,896]{1,0:T(8,128)(2,1)S(1)} %table_kernel.1.table_ref), custom_call_target="tpu_custom_call" | custom-call | tf_op jit(solution)/shard_map/transform_kernel/pallas_call | solution.py:267
  24.1 67.8 %all_to_all.10 = bf16[128,5,2,128]{3,2,1,0:T(2,128)(2,1)S(1)} all-to-all(bf16[128,5,2,128]{3,2,1,0:T(2,128)(2,1)S(1)} %bitcast.4), channel_id=1, replica_groups={{0,2,4,6,8,10,12,14,208,210,212,214,216,218,220,222,160,162,164,166,168..., dimensions={0} | all-to-all | bytes 655360 | tf_op jit(solution)/shard_map/all_to_all | solution.py:282
  91.9 1.5 %unpack_kernel.1 = (f32[12,8,1536]{2,1,0:T(8,128)}, f32[11,8,12]{2,1,0:T(8,128)}) custom-call(bf16[1280,128]{1,0:T(8,128)(2,1)S(1)} %bitcast.3), custom_call_target="tpu_custom_call" | custom-call | tf_op jit(solution)/shard_map/unpack_kernel/pallas_call | solution.py:286
Async XLA Ops:
  0.6 22.1 %all-to-all-start = ((bf16[8,96,192]{2,1,0:T(8,128)(2,1)}), bf16[8,96,192]{2,1,0:T(8,128)(2,1)S(1)}, u32[]{:S(2)}, u32[]{:S(2)}) async-start(bf16[8,96,192]{2,1,0:T(8,128)(2,1)} %param.1), calls=%async_computation | async-start | bytes 786432 | tf_op jit(solution)/shard_map/all_to_all | solution.py:256

commit v6 on v4

--- a/solution.py
+++ b/solution.py
@@ -14,7 +14,7 @@
 TILE = 2 * ROWS
 UNROLL = 4
 PACK_UNROLL = 16
-BAND_STEP = 13
+BAND_STEP = 3
 INTERPRET = False
 
 

time: 95.1 us -> 95.3 us (level); the launches traced: 93.3 us -> 95 us
  blocking collectives: 67.8 us -> 69.5 us
    all_to_all x1, blocking collectives: 67.8 us -> 69.5 us  [shards(): lax.all_to_all(packed, ('gy', 'gx'), split_axis=0, concat_axis=0, tiled=T...]
  transfers between devices with their start and end apart: 1 -> 1, of which waited for: 1 -> 1; matrix products, arithmetic and copies ran while one was open for 0% -> 0% of each run, Pallas kernels for 3% -> 2%
where the time goes in v6:
time: 95.3 us; the launch traced here: 95 us
  blocking collectives  69.5 us (73%)
  waiting for transfers between devices  12.4 us (13%)
  starting transfers between devices  7.33 us (8%)
  Pallas kernels  5.12 us (5%)
    all_to_all x1, blocking collectives, shards(): lax.all_to_all(packed, ('gy', 'gx'), split_axis=0, concat_axis=0, tiled=T...  69.5 us
    all_to_all x1, waiting for transfers between devices, shards(): lax.all_to_all(level_field, 'gx', split_axis=0, concat_axis=0, tiled=True)  12.4 us
    all_to_all x1, starting transfers between devices, shards(): lax.all_to_all(level_field, 'gx', split_axis=0, concat_axis=0, tiled=True)  7.33 us
    pallas_call x1, Pallas kernels, shards(): call(table_kernel, jax.ShapeDtypeStruct((coeffs + TILE, width), bf16), li...  2.33 us
  transfers between devices with their start and end apart: 1, of which 1 were waited for; matrix products, arithmetic and copies ran while one was open for 0% of the time, Pallas kernels for 2%

profile of v6, /device:TPU:80, one launch (start us, length us, event | category | flops | bytes accessed | tf_op | source)
XLA Modules:
  0.0 95.0 jit_solution(14864370530178192277)
XLA Ops:
  0.6 7.3 %all-to-all-start = ((bf16[8,96,192]{2,1,0:T(8,128)(2,1)}), bf16[8,96,192]{2,1,0:T(8,128)(2,1)S(1)}, u32[]{:S(2)}, u32[]{:S(2)}) async-start(bf16[8,96,192]{2,1,0:T(8,128)(2,1)} %param.1), calls=%async_computation | async-start | bytes 786432 | tf_op jit(solution)/shard_map/all_to_all | solution.py:258
  8.0 2.3 %table_kernel.1.table_ref = bf16[1552,896]{1,0:T(8,128)(2,1)S(1)} custom-call(), custom_call_target="tpu_custom_call" | custom-call | tf_op jit(solution)/shard_map/table_kernel/pallas_call | solution.py:260
  10.3 12.4 %all-to-all-done.core_ref = bf16[8,96,192]{2,1,0:T(8,128)(2,1)S(1)} async-done(((bf16[8,96,192]{2,1,0:T(8,128)(2,1)}), bf16[8,96,192]{2,1,0:T(8,128)(2,1)S(1)}, u32[]{:S(2)}, u32[]{:S(2)}) %all-to-all-start) | async-done | bytes 294944 | tf_op jit(solution)/shard_map/all_to_all | solution.py:258
  22.7 1.4 %transform_kernel.1 = bf16[1280,128]{1,0:T(8,128)(2,1)S(1)} custom-call(bf16[8,96,192]{2,1,0:T(8,128)(2,1)S(1)} %all-to-all-done.core_ref, bf16[1552,896]{1,0:T(8,128)(2,1)S(1)} %table_kernel.1.table_ref), custom_call_target="tpu_custom_call" | custom-call | tf_op jit(solution)/shard_map/transform_kernel/pallas_call | solution.py:269
  24.1 69.5 %all_to_all.10 = bf16[128,5,2,128]{3,2,1,0:T(2,128)(2,1)S(1)} all-to-all(bf16[128,5,2,128]{3,2,1,0:T(2,128)(2,1)S(1)} %bitcast.4), channel_id=1, replica_groups={{0,2,4,6,8,10,12,14,48,50,52,54,56,58,60,62,96,98,100,102,104,106,108,1..., dimensions={0} | all-to-all | bytes 655360 | tf_op jit(solution)/shard_map/all_to_all | solution.py:284
  93.6 1.4 %unpack_kernel.1 = (f32[12,8,1536]{2,1,0:T(8,128)}, f32[11,8,12]{2,1,0:T(8,128)}) custom-call(bf16[1280,128]{1,0:T(8,128)(2,1)S(1)} %bitcast.3), custom_call_target="tpu_custom_call" | custom-call | tf_op jit(solution)/shard_map/unpack_kernel/pallas_call | solution.py:288
Async XLA Ops:
  0.6 22.1 %all-to-all-start = ((bf16[8,96,192]{2,1,0:T(8,128)(2,1)}), bf16[8,96,192]{2,1,0:T(8,128)(2,1)S(1)}, u32[]{:S(2)}, u32[]{:S(2)}) async-start(bf16[8,96,192]{2,1,0:T(8,128)(2,1)} %param.1), calls=%async_computation | async-start | bytes 786432 | tf_op jit(solution)/shard_map/all_to_all | solution.py:258
